TPU v7x, 32 devices: a whole 2x2x4 slice. The times are simulated.
32 devices in a mesh: groups: 2 (over y), seq: 8 (over z, x), sub: 2 (over core).
Axes of the slice: x: 2, y: 2, z: 4, core: 2. Of those that a mesh axis runs over, the one named last changes fastest.
Arguments:
- cache_in: bfloat16 [64, 2, 36864], P('groups', None, ('sub', 'seq')), parts along dimension 0, may hold values from -6 to 6
- page_counts: int32 [16], P('groups'), parts along dimension 0, may hold values from 1 to 8, 32 in all
- tail_tokens: int32 [16], P('groups'), parts along dimension 0, may hold values from 1 to 64
- assignment: int32 [16], P('groups'), parts along dimension 0, may hold values from 0 to 7, each once
Outputs:
- cache_out: bfloat16 [128, 2, 36864], P(('groups', 'seq'), None, 'sub'), parts along dimension 0
- checksum: float32 [2, 128], P(None, ('groups', 'seq')), parts along dimension 1
There are 2 independent parts, one for each index of `groups`. A program takes and returns all parts, laid end to end along the dimension named above; each array names one. Nothing has to cross between parts.
Inputs may be any that keep to these rules, and one draw needn't show every extreme that they name: `page_counts`: the page counts sum to 32. `assignment`: every seq index serves exactly one request.
All inputs are finite; a program needn't handle non-finite values.
Results may differ from a plain program's by a relative error of at most 0.001.
Values may be sent and summed in bfloat16 or wider, within the bound.
A program may use at most 64 MiB of HBM per device.

v0:
```python
import functools

import jax
import jax.numpy as jnp
from jax import lax
from jax.experimental import pallas as pl
from jax.experimental.pallas import tpu as pltpu
from jax.sharding import PartitionSpec as P

LATENT = 576
PAGE = 64
MAXP = 8
LANES = 128
ROW_CHIPS = 2
MESH = pl.DeviceIdType.MESH


def by_device(matches, values):
    return jnp.sum(jnp.where(matches, values[None, :], 0), axis=1)


def general(cache_in, page_counts, tail_tokens, assignment):
    seq_count = lax.axis_size("seq")
    own_index = lax.axis_index("seq")
    sub_index = lax.axis_index("sub")
    total_pages, layer_count, piece = cache_in.shape
    starts = jnp.cumsum(page_counts) - page_counts
    device_ids = jnp.arange(seq_count, dtype=jnp.int32)
    matches = assignment[None, :] == device_ids[:, None]
    dest_counts = by_device(matches, page_counts)
    dest_starts = by_device(matches, starts)
    dest_tails = by_device(matches, tail_tokens)
    slot_ids = jnp.arange(seq_count * MAXP, dtype=jnp.int32)
    page_rank = slot_ids % MAXP
    counts_at = jnp.repeat(dest_counts, MAXP)
    starts_at = jnp.repeat(dest_starts, MAXP)
    tails_at = jnp.repeat(dest_tails, MAXP)
    in_use = page_rank < counts_at
    source_rows = jnp.where(in_use, starts_at + page_rank, 0)
    filled = jnp.where(in_use, jnp.where(page_rank < counts_at - 1, PAGE, tails_at), 0)
    column = (sub_index * seq_count + own_index) * piece + jnp.arange(piece, dtype=jnp.int32)
    token_of = column // LATENT
    kept_mask = token_of[None, :] < filled[:, None]
    zero_value = jnp.zeros((), cache_in.dtype)
    fetched = jnp.take(cache_in, source_rows, axis=0)
    packed = jnp.where(kept_mask[:, None, :], fetched, zero_value)
    cache_out = lax.all_to_all(packed, "seq", split_axis=0, concat_axis=2, tiled=True)
    squares = jnp.sum(jnp.square(cache_out.astype(jnp.float32)), axis=2)
    squares = lax.psum(squares, "sub")
    checksum = jnp.sqrt(1.0 + squares / (PAGE * LATENT)).T
    return (cache_out, checksum)


def exchange(n, subs, counts_in, tails_in, assign_in, x_in, out, chk, send, tab, part, parts_in,
             send_sem, recv_sem, psend_sem, precv_sem, ready_sem, own_sem, in_sem,
             x, counts, tails, assign):
    me = lax.axis_index("seq")
    sub = lax.axis_index("sub")
    pages, layers, piece = x.shape
    tokens = piece // LATENT
    own_id = me * subs + sub
    line = n // ROW_CHIPS
    z, col = me // ROW_CHIPS, me % ROW_CHIPS
    steps = [(dz, dx) for dx in range(ROW_CHIPS) for dz in range(1 - line, line) if dz or dx]
    steps.sort(key=lambda step: (-abs(step[0]), -step[1]))

    def inside(step):
        return jnp.logical_and(z + step[0] >= 0, z + step[0] < line)

    def peer(step):
        return (z + step[0]) * ROW_CHIPS + (col + step[1]) % ROW_CHIPS

    def device(other):
        return {"seq": other // subs, "sub": other % subs}

    everyone = range(n * subs)
    arrivals = [pltpu.make_async_copy(a, b, in_sem.at[k]) for k, (a, b) in enumerate(
        ((counts_in, counts), (tails_in, tails), (assign_in, assign), (x_in, x)))]
    for copy in arrivals:
        copy.start()
    barrier = pltpu.get_barrier_semaphore()
    for other in everyone:
        @pl.when(other > own_id)
        def _():
            pl.semaphore_signal(
                barrier, inc=1, device_id=device(other), device_id_type=MESH)

    column = lax.broadcasted_iota(jnp.int32, (layers, piece), 1)
    for f in range(tokens + 1):
        tab[f] = jnp.where(column < f * LATENT, 1.0, 0.0).astype(x.dtype)

    for copy in arrivals:
        copy.wait()
    reqs = counts.shape[0]
    packed, begin = [], jnp.int32(0)
    for r in range(reqs):
        packed.append((begin * 16 + counts[r]) * 128 + tails[r])
        begin = begin + counts[r]
    base = (sub * n + me) * tokens

    for dest in range(n):
        info = jnp.int32(0)
        for r in range(reqs):
            info = info + jnp.where(assign[r] == dest, packed[r], 0)
        tail = info & 127
        count = (info >> 7) & 15
        start = info >> 11
        for k in range(MAXP):
            used = k < count
            row = jnp.where(used, start + k, 0)
            filled = jnp.where(used, jnp.where(k < count - 1, PAGE, tail), 0)
            keep = jnp.clip(filled - base, 0, tokens)
            send[dest, k] = x[row] * tab[keep]

    def columns(source):
        return out.at[:, :, pl.ds(pl.multiple_of(source * piece, LANES), piece)]

    def piece_copy(dest, source):
        return pltpu.make_async_remote_copy(
            src_ref=send.at[dest],
            dst_ref=columns(source),
            send_sem=send_sem.at[dest],
            recv_sem=recv_sem.at[source],
            device_id={"seq": dest},
            device_id_type=MESH)

    def part_copy(i, j, source):
        dest = (me + i) % n
        return pltpu.make_async_remote_copy(
            src_ref=part.at[dest],
            dst_ref=parts_in.at[source],
            send_sem=psend_sem.at[i * subs + j],
            recv_sem=precv_sem.at[source],
            device_id={"seq": dest, "sub": (sub + j) % subs},
            device_id_type=MESH)

    own_copy = pltpu.make_async_copy(send.at[me], columns(me), own_sem)

    @pl.when(own_id > 0)
    def _():
        pl.semaphore_wait(barrier, own_id)

    for other in everyone:
        @pl.when(other < own_id)
        def _():
            pl.semaphore_signal(
                ready_sem.at[own_id], inc=1, device_id=device(other), device_id_type=MESH)
    for step in steps:
        @pl.when(jnp.logical_and(inside(step), peer(step) < me))
        def _():
            piece_copy(peer(step), me).start()
    own_copy.start()
    for dest in range(1, n):
        @pl.when(dest > me)
        def _():
            pl.semaphore_wait(ready_sem.at[dest * subs + sub], 1)
            piece_copy(dest, me).start()

    lane = lax.broadcasted_iota(jnp.int32, (layers, LANES), 1)
    for dest in range(n):
        total = jnp.zeros((layers, LANES), jnp.float32)
        for k in range(MAXP):
            v = send[dest, k].astype(jnp.float32)
            s = jnp.sum(v * v, axis=1, keepdims=True)
            total = jnp.where(lane == k, s, total)
        part[dest] = total
    parts_in[own_id] = part[me]
    for other in everyone:
        @pl.when(jnp.logical_and(other > own_id, other % subs != sub))
        def _():
            pl.semaphore_wait(ready_sem.at[other], 1)
    others = [(i, j) for i in range(n) for j in range(subs) if i or j]
    for i, j in others:
        part_copy(i, j, own_id).start()

    own_copy.wait()
    for i in range(1, n):
        pltpu.make_async_remote_copy(
            src_ref=send.at[(me + i) % n],
            dst_ref=columns((me + n - i) % n),
            send_sem=send_sem.at[(me + i) % n],
            recv_sem=recv_sem.at[(me + n - i) % n],
            device_id={"seq": (me + i) % n},
            device_id_type=MESH).wait()
    for i, j in others:
        part_copy(i, j, (me + n - i) % n * subs + (sub + subs - j) % subs).wait()
    total = jnp.sum(parts_in[...], axis=0)
    chk[...] = jnp.sqrt(1.0 + total / (PAGE * LATENT))[:, :MAXP]


def place(pages_in, sums_in, pages, sums, sem):
    copies = [pltpu.make_async_copy(a, b, sem.at[k]) for k, (a, b) in enumerate(
        ((pages_in, pages), (sums_in, sums)))]
    for copy in copies:
        copy.start()
    for copy in copies:
        copy.wait()


def direct(cache_in, page_counts, tail_tokens, assignment):
    n, subs = lax.axis_size("seq"), lax.axis_size("sub")
    pages, layers, piece = cache_in.shape
    vmem = pl.BlockSpec(memory_space=pltpu.VMEM)
    landed = pl.pallas_call(
        functools.partial(exchange, n, subs),
        out_shape=(pltpu.VMEM((MAXP, layers, piece * n), cache_in.dtype),
                   pltpu.VMEM((layers, MAXP), jnp.float32)),
        in_specs=[pl.BlockSpec(memory_space=pl.ANY)] * 4,
        out_specs=(vmem, vmem),
        scratch_shapes=[
            pltpu.VMEM((n, MAXP, layers, piece), cache_in.dtype),
            pltpu.VMEM((piece // LATENT + 1, layers, piece), cache_in.dtype),
            pltpu.VMEM((n, layers, LANES), jnp.float32),
            pltpu.VMEM((n * subs, layers, LANES), jnp.float32),
            pltpu.SemaphoreType.DMA((n,)),
            pltpu.SemaphoreType.DMA((n,)),
            pltpu.SemaphoreType.DMA((n * subs,)),
            pltpu.SemaphoreType.DMA((n * subs,)),
            pltpu.SemaphoreType.REGULAR((n * subs,)),
            pltpu.SemaphoreType.DMA,
            pltpu.SemaphoreType.DMA((4,)),
            pltpu.VMEM(cache_in.shape, cache_in.dtype),
            pltpu.SMEM(page_counts.shape, jnp.int32),
            pltpu.SMEM(page_counts.shape, jnp.int32),
            pltpu.SMEM(page_counts.shape, jnp.int32),
        ],
        compiler_params=pltpu.CompilerParams(collective_id=0, has_side_effects=True),
    )(page_counts, tail_tokens, assignment, cache_in)
    return pl.pallas_call(
        place,
        out_shape=tuple(jax.ShapeDtypeStruct(a.shape, a.dtype) for a in landed),
        in_specs=[vmem] * 2,
        out_specs=(pl.BlockSpec(memory_space=pltpu.HBM),) * 2,
        scratch_shapes=[pltpu.SemaphoreType.DMA((2,))],
    )(*(pltpu.with_memory_space_constraint(a, pltpu.VMEM) for a in landed))


def shards(cache_in, page_counts, tail_tokens, assignment):
    piece = cache_in.shape[2]
    whole_tiles = piece % LANES == 0 and piece % LATENT == 0 and lax.axis_size("seq") % ROW_CHIPS == 0
    return (direct if whole_tiles else general)(cache_in, page_counts, tail_tokens, assignment)


def solution(mesh):
    placed = (P("groups", None, ("sub", "seq")), P("groups"), P("groups"), P("groups"))
    return jax.shard_map(
        shards,
        mesh=mesh,
        in_specs=placed,
        out_specs=(P(("groups", "seq"), None, "sub"), P(None, ("groups", "seq"))),
        check_vma=False,
    )
```

profile of v0, /device:TPU:0, one launch (start us, length us, event | category | flops | bytes accessed | tf_op | source)
XLA Modules:
  0.0 22.4 jit_solution(3438238470118986704)
XLA Ops:
  0.6 21.0 %shard_map.59 = (bf16[8,2,18432]{2,1,0:T(2,128)(2,1)S(1)}, f32[2,8]{1,0:T(2,128)S(1)}) custom-call(s32[8]{0:T(128)} %counts_in.1, s32[8]{0:T(128)} %tails_in.1, s32[8]{0:T(128)} %assign_in.1, bf16[32,2,2304]{2,1,0:T(2,128)(2,1)} %x_in.1), custom_call_target="tpu_custom_call" | custom-call | tf_op jit(solution)/shard_map/pallas_call | solution.py:204
  21.6 0.8 %shard_map.60 = (bf16[8,2,18432]{2,1,0:T(2,128)(2,1)}, f32[2,8]{1,0:T(2,128)}) custom-call(bf16[8,2,18432]{2,1,0:T(2,128)(2,1)S(1)} %get-tuple-element.4.pages_in, f32[2,8]{1,0:T(2,128)S(1)} %get-tuple-element.5.sums_in), custom_call_target="tpu_custom_call" | custom-call | tf_op jit(solution)/shard_map/pallas_call | solution.py:229
where the time goes:
time: 22.6 us; the launch traced here: 22.4 us
  Pallas kernels  21.8 us (96%)
  between operations  0.64 us (3%)
    pallas_call x1, Pallas kernels, direct(): pl.pallas_call(functools.partial(exchange, n, subs), out_shape=(pltpu.VME...  21 us
    pallas_call x1, Pallas kernels, direct(): pl.pallas_call(place, out_shape=tuple((jax.ShapeDtypeStruct(a.shape, a.dt...  0.84 us

commit v1 on v0

--- a/solution.py
+++ b/solution.py
@@ -52,38 +52,39 @@
 
 
 def exchange(n, subs, counts_in, tails_in, assign_in, x_in, out, chk, send, tab, part, parts_in,
-             send_sem, recv_sem, psend_sem, precv_sem, ready_sem, own_sem, in_sem,
+             send_sem, recv_sem, psend_sem, precv_sem, ready_sem, in_sem,
              x, counts, tails, assign):
     me = lax.axis_index("seq")
     sub = lax.axis_index("sub")
     pages, layers, piece = x.shape
     tokens = piece // LATENT
+    line = n // ROW_CHIPS
+    mid = line // 2
+    row = ROW_CHIPS * subs
+    z, col = me // ROW_CHIPS, me % ROW_CHIPS
+    place_in_row = col * subs + sub
     own_id = me * subs + sub
-    line = n // ROW_CHIPS
-    z, col = me // ROW_CHIPS, me % ROW_CHIPS
-    steps = [(dz, dx) for dx in range(ROW_CHIPS) for dz in range(1 - line, line) if dz or dx]
-    steps.sort(key=lambda step: (-abs(step[0]), -step[1]))
-
-    def inside(step):
-        return jnp.logical_and(z + step[0] >= 0, z + step[0] < line)
-
-    def peer(step):
-        return (z + step[0]) * ROW_CHIPS + (col + step[1]) % ROW_CHIPS
-
-    def device(other):
-        return {"seq": other // subs, "sub": other % subs}
-
-    everyone = range(n * subs)
+
+    def device(level, spot):
+        return {"seq": level * ROW_CHIPS + spot // subs, "sub": spot % subs}
+
+    def early(level):
+        return jnp.logical_and(level == mid - 1, z == mid)
+
     arrivals = [pltpu.make_async_copy(a, b, in_sem.at[k]) for k, (a, b) in enumerate(
         ((counts_in, counts), (tails_in, tails), (assign_in, assign), (x_in, x)))]
     for copy in arrivals:
         copy.start()
     barrier = pltpu.get_barrier_semaphore()
-    for other in everyone:
-        @pl.when(other > own_id)
-        def _():
-            pl.semaphore_signal(
-                barrier, inc=1, device_id=device(other), device_id_type=MESH)
+    for level in range(line):
+        @pl.when(jnp.logical_or(level > z, early(level)))
+        def _():
+            for spot in range(row):
+                pl.semaphore_signal(
+                    barrier, inc=1, device_id=device(level, spot), device_id_type=MESH)
+    for j in range(1, row):
+        pl.semaphore_signal(
+            barrier, inc=1, device_id=device(z, (place_in_row + j) % row), device_id_type=MESH)
 
     column = lax.broadcasted_iota(jnp.int32, (layers, piece), 1)
     for f in range(tokens + 1):
@@ -107,54 +108,49 @@
         start = info >> 11
         for k in range(MAXP):
             used = k < count
-            row = jnp.where(used, start + k, 0)
+            row_at = jnp.where(used, start + k, 0)
             filled = jnp.where(used, jnp.where(k < count - 1, PAGE, tail), 0)
             keep = jnp.clip(filled - base, 0, tokens)
-            send[dest, k] = x[row] * tab[keep]
+            send[dest, k] = x[row_at] * tab[keep]
 
     def columns(source):
         return out.at[:, :, pl.ds(pl.multiple_of(source * piece, LANES), piece)]
 
-    def piece_copy(dest, source):
-        return pltpu.make_async_remote_copy(
+    def send_piece(level, place):
+        dest = level * ROW_CHIPS + place
+        pltpu.make_async_remote_copy(
             src_ref=send.at[dest],
-            dst_ref=columns(source),
-            send_sem=send_sem.at[dest],
-            recv_sem=recv_sem.at[source],
+            dst_ref=columns(me),
+            send_sem=send_sem,
+            recv_sem=recv_sem,
             device_id={"seq": dest},
-            device_id_type=MESH)
-
-    def part_copy(i, j, source):
-        dest = (me + i) % n
-        return pltpu.make_async_remote_copy(
-            src_ref=part.at[dest],
-            dst_ref=parts_in.at[source],
-            send_sem=psend_sem.at[i * subs + j],
-            recv_sem=precv_sem.at[source],
-            device_id={"seq": dest, "sub": (sub + j) % subs},
-            device_id_type=MESH)
-
-    own_copy = pltpu.make_async_copy(send.at[me], columns(me), own_sem)
-
-    @pl.when(own_id > 0)
+            device_id_type=MESH).start()
+
+    def send_part(level, spot):
+        pltpu.make_async_remote_copy(
+            src_ref=part.at[level * ROW_CHIPS + spot // subs],
+            dst_ref=parts_in.at[own_id],
+            send_sem=psend_sem,
+            recv_sem=precv_sem,
+            device_id=device(level, spot),
+            device_id_type=MESH).start()
+
+    pl.semaphore_wait(barrier, (z + 1) * row - 1 + jnp.where(z == mid - 1, row, 0))
+    for level in range(line - 1):
+        @pl.when(jnp.logical_and(level < z, jnp.logical_not(early(level))))
+        def _():
+            for spot in range(row):
+                pl.semaphore_signal(
+                    ready_sem.at[z], inc=1, device_id=device(level, spot), device_id_type=MESH)
+
+    @pl.when(z > 0)
     def _():
-        pl.semaphore_wait(barrier, own_id)
-
-    for other in everyone:
-        @pl.when(other < own_id)
-        def _():
-            pl.semaphore_signal(
-                ready_sem.at[own_id], inc=1, device_id=device(other), device_id_type=MESH)
-    for step in steps:
-        @pl.when(jnp.logical_and(inside(step), peer(step) < me))
-        def _():
-            piece_copy(peer(step), me).start()
-    own_copy.start()
-    for dest in range(1, n):
-        @pl.when(dest > me)
-        def _():
-            pl.semaphore_wait(ready_sem.at[dest * subs + sub], 1)
-            piece_copy(dest, me).start()
+        for i in range(ROW_CHIPS):
+            send_piece(0, (col + i) % ROW_CHIPS)
+
+    @pl.when(z == mid - 1)
+    def _():
+        send_piece(mid, col)
 
     lane = lax.broadcasted_iota(jnp.int32, (layers, LANES), 1)
     for dest in range(n):
@@ -164,28 +160,54 @@
             s = jnp.sum(v * v, axis=1, keepdims=True)
             total = jnp.where(lane == k, s, total)
         part[dest] = total
+    mine = pl.ds(pl.multiple_of(me * piece, LANES), piece)
+    for k in range(MAXP):
+        out[k, :, mine] = send[me, k]
     parts_in[own_id] = part[me]
-    for other in everyone:
-        @pl.when(jnp.logical_and(other > own_id, other % subs != sub))
-        def _():
-            pl.semaphore_wait(ready_sem.at[other], 1)
-    others = [(i, j) for i in range(n) for j in range(subs) if i or j]
-    for i, j in others:
-        part_copy(i, j, own_id).start()
-
-    own_copy.wait()
-    for i in range(1, n):
-        pltpu.make_async_remote_copy(
-            src_ref=send.at[(me + i) % n],
-            dst_ref=columns((me + n - i) % n),
-            send_sem=send_sem.at[(me + i) % n],
-            recv_sem=recv_sem.at[(me + n - i) % n],
-            device_id={"seq": (me + i) % n},
-            device_id_type=MESH).wait()
-    for i, j in others:
-        part_copy(i, j, (me + n - i) % n * subs + (sub + subs - j) % subs).wait()
+
+    for level in range(line - 1):
+        @pl.when(level < z)
+        def _():
+            for spot in range(row):
+                send_part(level, spot)
+    for j in range(1, row):
+        send_part(z, (place_in_row + j) % row)
+
+    @pl.when(z == mid - 1)
+    def _():
+        for spot in range(row):
+            send_part(mid, spot)
+        for i in range(1, ROW_CHIPS):
+            send_piece(mid, (col + i) % ROW_CHIPS)
+
+    for level in range(1, line - 1):
+        @pl.when(level < z)
+        def _():
+            for i in range(ROW_CHIPS):
+                send_piece(level, (col + i) % ROW_CHIPS)
+    for i in range(1, ROW_CHIPS):
+        send_piece(z, (col + i) % ROW_CHIPS)
+
+    for level in range(1, line):
+        special = jnp.logical_and(z == mid - 1, level == mid)
+        @pl.when(jnp.logical_and(level > z, jnp.logical_not(special)))
+        def _():
+            pl.semaphore_wait(ready_sem.at[level], row)
+            for spot in range(row):
+                send_part(level, spot)
+            for i in range(ROW_CHIPS):
+                send_piece(level, (col + i) % ROW_CHIPS)
+
+    def whole(ref, sem):
+        return pltpu.make_async_copy(ref, ref, sem)
+
+    others = n * subs - 1
+    whole(parts_in.at[pl.ds(0, others)], precv_sem).wait()
     total = jnp.sum(parts_in[...], axis=0)
     chk[...] = jnp.sqrt(1.0 + total / (PAGE * LATENT))[:, :MAXP]
+    whole(parts_in.at[pl.ds(0, others)], psend_sem).wait()
+    whole(send.at[pl.ds(0, n - 1)], send_sem).wait()
+    whole(send.at[pl.ds(0, n - 1)], recv_sem).wait()
 
 
 def place(pages_in, sums_in, pages, sums, sem):
@@ -212,12 +234,11 @@
             pltpu.VMEM((piece // LATENT + 1, layers, piece), cache_in.dtype),
             pltpu.VMEM((n, layers, LANES), jnp.float32),
             pltpu.VMEM((n * subs, layers, LANES), jnp.float32),
-            pltpu.SemaphoreType.DMA((n,)),
-            pltpu.SemaphoreType.DMA((n,)),
-            pltpu.SemaphoreType.DMA((n * subs,)),
-            pltpu.SemaphoreType.DMA((n * subs,)),
-            pltpu.SemaphoreType.REGULAR((n * subs,)),
-            pltpu.SemaphoreType.DMA,
+            pltpu.SemaphoreType.DMA,
+            pltpu.SemaphoreType.DMA,
+            pltpu.SemaphoreType.DMA,
+            pltpu.SemaphoreType.DMA,
+            pltpu.SemaphoreType.REGULAR((n // ROW_CHIPS,)),
             pltpu.SemaphoreType.DMA((4,)),
             pltpu.VMEM(cache_in.shape, cache_in.dtype),
             pltpu.SMEM(page_counts.shape, jnp.int32),

time: 22.6 us -> 19.5 us (0.86)
  the two profiles are of different devices: /device:TPU:0 before, /device:TPU:8 now
where the time goes in v1:
time: 19.5 us; the launch traced here: 19.2 us
  Pallas kernels  18.6 us (95%)
  between operations  0.64 us (3%)
    pallas_call x1, Pallas kernels, direct(): pl.pallas_call(functools.partial(exchange, n, subs), out_shape=(pltpu.VME...  17.7 us
    pallas_call x1, Pallas kernels, direct(): pl.pallas_call(place, out_shape=tuple((jax.ShapeDtypeStruct(a.shape, a.dt...  0.84 us

profile of v1, /device:TPU:8, one launch (start us, length us, event | category | flops | bytes accessed | tf_op | source)
XLA Modules:
  0.0 19.2 jit_solution(7164241854248701037)
XLA Ops:
  0.6 17.7 %shard_map.59 = (bf16[8,2,18432]{2,1,0:T(2,128)(2,1)S(1)}, f32[2,8]{1,0:T(2,128)S(1)}) custom-call(s32[8]{0:T(128)} %counts_in.1, s32[8]{0:T(128)} %tails_in.1, s32[8]{0:T(128)} %assign_in.1, bf16[32,2,2304]{2,1,0:T(2,128)(2,1)} %x_in.1), custom_call_target="tpu_custom_call" | custom-call | tf_op jit(solution)/shard_map/pallas_call | solution.py:226
  18.4 0.8 %shard_map.60 = (bf16[8,2,18432]{2,1,0:T(2,128)(2,1)}, f32[2,8]{1,0:T(2,128)}) custom-call(bf16[8,2,18432]{2,1,0:T(2,128)(2,1)S(1)} %get-tuple-element.4.pages_in, f32[2,8]{1,0:T(2,128)S(1)} %get-tuple-element.5.sums_in), custom_call_target="tpu_custom_call" | custom-call | tf_op jit(solution)/shard_map/pallas_call | solution.py:250

commit v2 on v1

--- a/solution.py
+++ b/solution.py
@@ -12,6 +12,8 @@
 MAXP = 8
 LANES = 128
 ROW_CHIPS = 2
+NEAR_DIRECT = 8
+FAR_DIRECT = 4
 MESH = pl.DeviceIdType.MESH
 
 
@@ -51,19 +53,37 @@
     return (cache_out, checksum)
 
 
+def kept_direct(away):
+    return FAR_DIRECT if away else NEAR_DIRECT
+
+
+def most_spilled(pages, n, direct):
+    half = n // 2
+    room = min(pages - half, half * MAXP)
+    full, rest = room // MAXP, room % MAXP
+    return (MAXP - direct) * full + max(0, rest - direct)
+
+
 def exchange(n, subs, counts_in, tails_in, assign_in, x_in, out, chk, send, tab, part, parts_in,
              send_sem, recv_sem, psend_sem, precv_sem, ready_sem, in_sem,
-             x, counts, tails, assign):
+             x, counts, tails, assign, rsend_sem, spill_sem, relay, *spills):
     me = lax.axis_index("seq")
     sub = lax.axis_index("sub")
     pages, layers, piece = x.shape
     tokens = piece // LATENT
     line = n // ROW_CHIPS
     mid = line // 2
+    half = mid * ROW_CHIPS
+    spilled = [most_spilled(pages, n, kept_direct(away)) for away in range(mid)]
+    spill, landed = spills[0], spills[1:]
     row = ROW_CHIPS * subs
     z, col = me // ROW_CHIPS, me % ROW_CHIPS
     place_in_row = col * subs + sub
     own_id = me * subs + sub
+    upper = z // mid
+    own_first = upper * half
+    far_first = half - own_first
+    relays = jnp.logical_or(z == mid - 1, z == mid)
 
     def device(level, spot):
         return {"seq": level * ROW_CHIPS + spot // subs, "sub": spot % subs}
@@ -89,6 +109,8 @@
     column = lax.broadcasted_iota(jnp.int32, (layers, piece), 1)
     for f in range(tokens + 1):
         tab[f] = jnp.where(column < f * LATENT, 1.0, 0.0).astype(x.dtype)
+    for away in range(mid):
+        landed[away][spilled[away]] = jnp.zeros((layers, piece), x.dtype)
 
     for copy in arrivals:
         copy.wait()
@@ -99,10 +121,14 @@
         begin = begin + counts[r]
     base = (sub * n + me) * tokens
 
-    for dest in range(n):
+    def request_of(dest):
         info = jnp.int32(0)
         for r in range(reqs):
             info = info + jnp.where(assign[r] == dest, packed[r], 0)
+        return info
+
+    for dest in range(n):
+        info = request_of(dest)
         tail = info & 127
         count = (info >> 7) & 15
         start = info >> 11
@@ -111,20 +137,68 @@
             row_at = jnp.where(used, start + k, 0)
             filled = jnp.where(used, jnp.where(k < count - 1, PAGE, tail), 0)
             keep = jnp.clip(filled - base, 0, tokens)
-            send[dest, k] = x[row_at] * tab[keep]
-
-    def columns(source):
-        return out.at[:, :, pl.ds(pl.multiple_of(source * piece, LANES), piece)]
-
-    def send_piece(level, place):
+            send[dest * MAXP + k] = x[row_at] * tab[keep]
+
+    def whole(ref, sem):
+        return pltpu.make_async_copy(ref, ref, sem)
+
+    def away_of(level):
+        return level - mid if level >= mid else mid - 1 - level
+
+    def spill_starts(first, direct):
+        starts, begin = [], jnp.int32(0)
+        for j in range(half):
+            count = (request_of(first + j) >> 7) & 15
+            starts.append((begin, count))
+            begin = begin + jnp.maximum(count - direct, 0)
+        return starts
+
+    for level in range(line):
+        size, direct = spilled[away_of(level)], kept_direct(away_of(level))
+        if not size:
+            continue
+
+        @pl.when(z == level)
+        def _():
+            far = spill_starts(far_first, direct)
+            for o in range(size):
+                at = direct + o
+                for j in range(1, half):
+                    at = jnp.where(o >= far[j][0], j * MAXP + direct + o - far[j][0], at)
+                spill[o] = send[far_first * MAXP + jnp.minimum(at, half * MAXP - 1)]
+
+    def columns(source, first=0, rows=MAXP):
+        return out.at[pl.ds(first, rows), :, pl.ds(pl.multiple_of(source * piece, LANES), piece)]
+
+    def rows_to(zz, level):
+        return MAXP if zz // mid == level // mid else kept_direct(away_of(zz))
+
+    def send_piece(zz, level, turn):
+        place = turn if level == 0 else (col + 1 + sub + turn) % ROW_CHIPS
         dest = level * ROW_CHIPS + place
+        rows = rows_to(zz, level)
         pltpu.make_async_remote_copy(
-            src_ref=send.at[dest],
-            dst_ref=columns(me),
+            src_ref=send.at[pl.ds(dest * MAXP, rows)],
+            dst_ref=columns(me, 0, rows),
             send_sem=send_sem,
             recv_sem=recv_sem,
             device_id={"seq": dest},
             device_id_type=MESH).start()
+
+    def send_row(zz, level):
+        for turn in range(ROW_CHIPS):
+            send_piece(zz, level, turn)
+
+    def send_spill(zz, level):
+        away = away_of(zz)
+        if spilled[away]:
+            pltpu.make_async_remote_copy(
+                src_ref=spill.at[pl.ds(0, spilled[away])],
+                dst_ref=landed[away].at[pl.ds(0, spilled[away])],
+                send_sem=send_sem,
+                recv_sem=spill_sem.at[away],
+                device_id={"seq": level * ROW_CHIPS + col},
+                device_id_type=MESH).start()
 
     def send_part(level, spot):
         pltpu.make_async_remote_copy(
@@ -135,6 +209,58 @@
             device_id=device(level, spot),
             device_id_type=MESH).start()
 
+    def send_parts(level):
+        for spot in range(row):
+            send_part(level, spot)
+
+    def sends_first(zz):
+        if zz >= mid:
+            send_spill(zz, mid - 1)
+        if zz == mid - 1:
+            send_spill(zz, mid)
+        if zz >= mid:
+            send_row(zz, 0)
+        if zz == mid - 1:
+            send_row(zz, mid)
+
+    def sends_later(zz):
+        for level in range(zz):
+            send_parts(level)
+        for j in range(1, row):
+            send_part(zz, (place_in_row + j) % row)
+        dest = zz * ROW_CHIPS + (col + 1) % ROW_CHIPS
+        pltpu.make_async_remote_copy(
+            src_ref=send.at[pl.ds(dest * MAXP, MAXP)],
+            dst_ref=columns(me),
+            send_sem=send_sem,
+            recv_sem=recv_sem,
+            device_id={"seq": dest},
+            device_id_type=MESH).start()
+        if zz == mid - 1:
+            send_parts(mid)
+        if 0 < zz < mid:
+            send_row(zz, 0)
+        first = mid if zz >= mid else 1
+        for level in range(zz - 1, first - 1, -1):
+            send_row(zz, level)
+        if zz >= mid:
+            for level in range(1, mid):
+                send_row(zz, level)
+        for level in range(zz + 1, line):
+            if (zz, level) != (mid - 1, mid):
+                pl.semaphore_wait(ready_sem.at[level], row)
+                send_parts(level)
+            if level < mid:
+                send_piece(zz, level, 0)
+            elif zz >= mid or level > mid:
+                send_row(zz, level)
+            elif zz != mid - 1:
+                send_spill(zz, mid)
+        for level in range(zz + 1, mid):
+            send_piece(zz, level, 1)
+        if zz < mid - 1:
+            send_row(zz, mid)
+
     pl.semaphore_wait(barrier, (z + 1) * row - 1 + jnp.where(z == mid - 1, row, 0))
     for level in range(line - 1):
         @pl.when(jnp.logical_and(level < z, jnp.logical_not(early(level))))
@@ -143,71 +269,82 @@
                 pl.semaphore_signal(
                     ready_sem.at[z], inc=1, device_id=device(level, spot), device_id_type=MESH)
 
-    @pl.when(z > 0)
-    def _():
-        for i in range(ROW_CHIPS):
-            send_piece(0, (col + i) % ROW_CHIPS)
-
-    @pl.when(z == mid - 1)
-    def _():
-        send_piece(mid, col)
+    for level in range(line):
+        @pl.when(z == level)
+        def _():
+            sends_first(level)
 
     lane = lax.broadcasted_iota(jnp.int32, (layers, LANES), 1)
     for dest in range(n):
         total = jnp.zeros((layers, LANES), jnp.float32)
         for k in range(MAXP):
-            v = send[dest, k].astype(jnp.float32)
+            v = send[dest * MAXP + k].astype(jnp.float32)
             s = jnp.sum(v * v, axis=1, keepdims=True)
             total = jnp.where(lane == k, s, total)
         part[dest] = total
     mine = pl.ds(pl.multiple_of(me * piece, LANES), piece)
     for k in range(MAXP):
-        out[k, :, mine] = send[me, k]
+        out[k, :, mine] = send[me * MAXP + k]
     parts_in[own_id] = part[me]
 
-    for level in range(line - 1):
-        @pl.when(level < z)
-        def _():
-            for spot in range(row):
-                send_part(level, spot)
-    for j in range(1, row):
-        send_part(z, (place_in_row + j) % row)
-
-    @pl.when(z == mid - 1)
-    def _():
-        for spot in range(row):
-            send_part(mid, spot)
-        for i in range(1, ROW_CHIPS):
-            send_piece(mid, (col + i) % ROW_CHIPS)
-
-    for level in range(1, line - 1):
-        @pl.when(level < z)
-        def _():
-            for i in range(ROW_CHIPS):
-                send_piece(level, (col + i) % ROW_CHIPS)
-    for i in range(1, ROW_CHIPS):
-        send_piece(z, (col + i) % ROW_CHIPS)
-
-    for level in range(1, line):
-        special = jnp.logical_and(z == mid - 1, level == mid)
-        @pl.when(jnp.logical_and(level > z, jnp.logical_not(special)))
-        def _():
-            pl.semaphore_wait(ready_sem.at[level], row)
-            for spot in range(row):
-                send_part(level, spot)
-            for i in range(ROW_CHIPS):
-                send_piece(level, (col + i) % ROW_CHIPS)
-
-    def whole(ref, sem):
-        return pltpu.make_async_copy(ref, ref, sem)
+    for level in range(line):
+        @pl.when(z == level)
+        def _():
+            sends_later(level)
+
+    for away in range(mid - 1, -1, -1):
+        size, direct = spilled[away], kept_direct(away)
+        rest = MAXP - direct
+        if not size:
+            continue
+
+        @pl.when(relays)
+        def _():
+            near = spill_starts(own_first, direct)
+            level = jnp.where(upper == 1, mid - 1 - away, mid + away)
+            source = level * ROW_CHIPS + col
+            whole(landed[away].at[pl.ds(0, size)], spill_sem.at[away]).wait()
+            for j in range(half):
+                for k in range(rest):
+                    at = jnp.where(k + direct < near[j][1], near[j][0] + k, size)
+                    relay[away, j * rest + k] = landed[away][at]
+            kept = columns(source, direct, rest)
+            for j in range(half):
+                @pl.when(own_first + j != me)
+                def _():
+                    pltpu.make_async_remote_copy(
+                        src_ref=relay.at[away, pl.ds(j * rest, rest)],
+                        dst_ref=kept,
+                        send_sem=rsend_sem,
+                        recv_sem=recv_sem,
+                        device_id={"seq": own_first + j},
+                        device_id_type=MESH).start()
+            at_source = pl.ds(pl.multiple_of(source * piece, LANES), piece)
+            for k in range(rest):
+                out[direct + k, :, at_source] = relay[away, (me - own_first) * rest + k]
 
     others = n * subs - 1
     whole(parts_in.at[pl.ds(0, others)], precv_sem).wait()
     total = jnp.sum(parts_in[...], axis=0)
     chk[...] = jnp.sqrt(1.0 + total / (PAGE * LATENT))[:, :MAXP]
     whole(parts_in.at[pl.ds(0, others)], psend_sem).wait()
-    whole(send.at[pl.ds(0, n - 1)], send_sem).wait()
-    whole(send.at[pl.ds(0, n - 1)], recv_sem).wait()
+    for level in range(line):
+        away = away_of(level)
+        sent = (half - 1) * MAXP + half * kept_direct(away)
+        got = (half - 1) * MAXP + half * MAXP
+        if away == 0:
+            got -= sum(MAXP - kept_direct(a) for a in range(mid))
+
+        @pl.when(z == level)
+        def _():
+            whole(send.at[pl.ds(0, sent)], send_sem).wait()
+            if spilled[away]:
+                whole(spill.at[pl.ds(0, spilled[away])], send_sem).wait()
+            if away == 0:
+                for a in range(mid):
+                    if spilled[a]:
+                        whole(send.at[pl.ds(0, (half - 1) * (MAXP - kept_direct(a)))], rsend_sem).wait()
+            whole(send.at[pl.ds(0, got)], recv_sem).wait()
 
 
 def place(pages_in, sums_in, pages, sums, sem):
@@ -222,6 +359,8 @@
 def direct(cache_in, page_counts, tail_tokens, assignment):
     n, subs = lax.axis_size("seq"), lax.axis_size("sub")
     pages, layers, piece = cache_in.shape
+    mid = n // ROW_CHIPS // 2
+    spilled = [most_spilled(pages, n, kept_direct(away)) for away in range(mid)]
     vmem = pl.BlockSpec(memory_space=pltpu.VMEM)
     landed = pl.pallas_call(
         functools.partial(exchange, n, subs),
@@ -230,7 +369,7 @@
         in_specs=[pl.BlockSpec(memory_space=pl.ANY)] * 4,
         out_specs=(vmem, vmem),
         scratch_shapes=[
-            pltpu.VMEM((n, MAXP, layers, piece), cache_in.dtype),
+            pltpu.VMEM((n * MAXP, layers, piece), cache_in.dtype),
             pltpu.VMEM((piece // LATENT + 1, layers, piece), cache_in.dtype),
             pltpu.VMEM((n, layers, LANES), jnp.float32),
             pltpu.VMEM((n * subs, layers, LANES), jnp.float32),
@@ -244,7 +383,11 @@
             pltpu.SMEM(page_counts.shape, jnp.int32),
             pltpu.SMEM(page_counts.shape, jnp.int32),
             pltpu.SMEM(page_counts.shape, jnp.int32),
-        ],
+            pltpu.SemaphoreType.DMA,
+            pltpu.SemaphoreType.DMA((mid,)),
+            pltpu.VMEM((mid, n // 2 * MAXP, layers, piece), cache_in.dtype),
+            pltpu.VMEM((max(spilled) + 1, layers, piece), cache_in.dtype),
+        ] + [pltpu.VMEM((size + 1, layers, piece), cache_in.dtype) for size in spilled],
         compiler_params=pltpu.CompilerParams(collective_id=0, has_side_effects=True),
     )(page_counts, tail_tokens, assignment, cache_in)
     return pl.pallas_call(
@@ -258,7 +401,7 @@
 
 def shards(cache_in, page_counts, tail_tokens, assignment):
     piece = cache_in.shape[2]
-    whole_tiles = piece % LANES == 0 and piece % LATENT == 0 and lax.axis_size("seq") % ROW_CHIPS == 0
+    whole_tiles = piece % LANES == 0 and piece % LATENT == 0 and lax.axis_size("seq") % (2 * ROW_CHIPS) == 0
     return (direct if whole_tiles else general)(cache_in, page_counts, tail_tokens, assignment)
 
 

time: 19.5 us -> 18.2 us (0.933)
  Pallas kernels: 18.6 us -> 17.4 us
    pallas_call x1, Pallas kernels: 17.7 us -> 16.5 us  [direct(): pl.pallas_call(functools.partial(exchange, n, subs), out_shape=(pltpu.VME...]
where the time goes in v2:
time: 18.2 us; the launch traced here: 18 us
  Pallas kernels  17.4 us (96%)
  between operations  0.64 us (4%)
    pallas_call x1, Pallas kernels, direct(): pl.pallas_call(functools.partial(exchange, n, subs), out_shape=(pltpu.VME...  16.5 us
    pallas_call x1, Pallas kernels, direct(): pl.pallas_call(place, out_shape=tuple((jax.ShapeDtypeStruct(a.shape, a.dt...  0.84 us

profile of v2, /device:TPU:8, one launch (start us, length us, event | category | flops | bytes accessed | tf_op | source)
XLA Modules:
  0.0 18.0 jit_solution(13737613231794384186)
XLA Ops:
  0.6 16.5 %shard_map.59 = (bf16[8,2,18432]{2,1,0:T(2,128)(2,1)S(1)}, f32[2,8]{1,0:T(2,128)S(1)}) custom-call(s32[8]{0:T(128)} %counts_in.1, s32[8]{0:T(128)} %tails_in.1, s32[8]{0:T(128)} %assign_in.1, bf16[32,2,2304]{2,1,0:T(2,128)(2,1)} %x_in.1), custom_call_target="tpu_custom_call" | custom-call | tf_op jit(solution)/shard_map/pallas_call | solution.py:365
  17.2 0.8 %shard_map.60 = (bf16[8,2,18432]{2,1,0:T(2,128)(2,1)}, f32[2,8]{1,0:T(2,128)}) custom-call(bf16[8,2,18432]{2,1,0:T(2,128)(2,1)S(1)} %get-tuple-element.4.pages_in, f32[2,8]{1,0:T(2,128)S(1)} %get-tuple-element.5.sums_in), custom_call_target="tpu_custom_call" | custom-call | tf_op jit(solution)/shard_map/pallas_call | solution.py:393

commit v3 on v2

--- a/solution.py
+++ b/solution.py
@@ -14,6 +14,9 @@
 ROW_CHIPS = 2
 NEAR_DIRECT = 8
 FAR_DIRECT = 4
+SPILL, RELAY = 8, 9
+ORDER = [[[1, 3, 8, 7, 6, 2, 5, 4], [1, 2, 8, 6, 7, 3, 4, 5], [0, 2, 8, 6, 7, 3, 4, 5], [0, 3, 8, 7, 6, 2, 5, 4]], [[4, 5, 3, 0, 7, 6, 9, 1], [4, 5, 3, 0, 6, 7, 9, 1], [5, 4, 2, 0, 6, 7, 9, 1], [5, 4, 2, 0, 7, 6, 9, 1]], [[0, 1, 3, 2, 7, 6, 5, 9], [0, 1, 3, 2, 6, 7, 5, 9], [1, 0, 2, 3, 6, 7, 4, 9], [1, 0, 2, 3, 7, 6, 4, 9]], [[8, 0, 1, 7, 5, 4, 3, 2], [8, 0, 1, 7, 4, 5, 2, 3], [8, 0, 1, 6, 4, 5, 2, 3], [8, 0, 1, 6, 5, 4, 3, 2]]]
+EARLY = [0, 1, 1, 3]
 MESH = pl.DeviceIdType.MESH
 
 
@@ -65,7 +68,7 @@
 
 
 def exchange(n, subs, counts_in, tails_in, assign_in, x_in, out, chk, send, tab, part, parts_in,
-             send_sem, recv_sem, psend_sem, precv_sem, ready_sem, in_sem,
+             send_sem, recv_sem, psend_sem, precv_sem, ready_sem, mate_sem, in_sem,
              x, counts, tails, assign, rsend_sem, spill_sem, relay, *spills):
     me = lax.axis_index("seq")
     sub = lax.axis_index("sub")
@@ -83,28 +86,37 @@
     upper = z // mid
     own_first = upper * half
     far_first = half - own_first
-    relays = jnp.logical_or(z == mid - 1, z == mid)
+    central = jnp.logical_or(z == mid - 1, z == mid)
 
     def device(level, spot):
         return {"seq": level * ROW_CHIPS + spot // subs, "sub": spot % subs}
-
-    def early(level):
-        return jnp.logical_and(level == mid - 1, z == mid)
 
     arrivals = [pltpu.make_async_copy(a, b, in_sem.at[k]) for k, (a, b) in enumerate(
         ((counts_in, counts), (tails_in, tails), (assign_in, assign), (x_in, x)))]
     for copy in arrivals:
         copy.start()
     barrier = pltpu.get_barrier_semaphore()
+    def greet(level, spot):
+        pl.semaphore_signal(
+            barrier, inc=1, device_id=device(level, spot), device_id_type=MESH)
+
     for level in range(line):
-        @pl.when(jnp.logical_or(level > z, early(level)))
+        @pl.when(z < level)
         def _():
-            for spot in range(row):
-                pl.semaphore_signal(
-                    barrier, inc=1, device_id=device(level, spot), device_id_type=MESH)
-    for j in range(1, row):
-        pl.semaphore_signal(
-            barrier, inc=1, device_id=device(z, (place_in_row + j) % row), device_id_type=MESH)
+            for spot in range(subs if level == mid else row):
+                greet(level, spot + col * subs if level == mid else spot)
+
+    @pl.when(z == mid)
+    def _():
+        for spot in range(subs):
+            greet(mid - 1, col * subs + spot)
+        for j in range(1, subs):
+            greet(z, col * subs + (sub + j) % subs)
+
+    @pl.when(z != mid)
+    def _():
+        for j in range(1, row):
+            greet(z, (place_in_row + j) % row)
 
     column = lax.broadcasted_iota(jnp.int32, (layers, piece), 1)
     for f in range(tokens + 1):
@@ -127,7 +139,10 @@
             info = info + jnp.where(assign[r] == dest, packed[r], 0)
         return info
 
-    for dest in range(n):
+    ahead = jnp.where(z == mid - 1, half, 0) + jnp.where(central, col, 0)
+
+    def fill(turn):
+        dest = (ahead + turn) % n
         info = request_of(dest)
         tail = info & 127
         count = (info >> 7) & 15
@@ -153,28 +168,13 @@
             begin = begin + jnp.maximum(count - direct, 0)
         return starts
 
-    for level in range(line):
-        size, direct = spilled[away_of(level)], kept_direct(away_of(level))
-        if not size:
-            continue
-
-        @pl.when(z == level)
-        def _():
-            far = spill_starts(far_first, direct)
-            for o in range(size):
-                at = direct + o
-                for j in range(1, half):
-                    at = jnp.where(o >= far[j][0], j * MAXP + direct + o - far[j][0], at)
-                spill[o] = send[far_first * MAXP + jnp.minimum(at, half * MAXP - 1)]
-
     def columns(source, first=0, rows=MAXP):
         return out.at[pl.ds(first, rows), :, pl.ds(pl.multiple_of(source * piece, LANES), piece)]
 
     def rows_to(zz, level):
         return MAXP if zz // mid == level // mid else kept_direct(away_of(zz))
 
-    def send_piece(zz, level, turn):
-        place = turn if level == 0 else (col + 1 + sub + turn) % ROW_CHIPS
+    def send_piece(zz, level, place):
         dest = level * ROW_CHIPS + place
         rows = rows_to(zz, level)
         pltpu.make_async_remote_copy(
@@ -187,7 +187,7 @@
 
     def send_row(zz, level):
         for turn in range(ROW_CHIPS):
-            send_piece(zz, level, turn)
+            send_piece(zz, level, (col + 1 + sub + turn) % ROW_CHIPS)
 
     def send_spill(zz, level):
         away = away_of(zz)
@@ -213,21 +213,15 @@
         for spot in range(row):
             send_part(level, spot)
 
-    def sends_first(zz):
-        if zz >= mid:
-            send_spill(zz, mid - 1)
-        if zz == mid - 1:
-            send_spill(zz, mid)
-        if zz >= mid:
-            send_row(zz, 0)
-        if zz == mid - 1:
-            send_row(zz, mid)
-
-    def sends_later(zz):
-        for level in range(zz):
-            send_parts(level)
-        for j in range(1, row):
-            send_part(zz, (place_in_row + j) % row)
+    def tell_lower():
+        for level in range(line - 1):
+            @pl.when(jnp.logical_and(level < z, jnp.logical_not(jnp.logical_and(level == mid - 1, z == mid))))
+            def _():
+                for spot in range(row):
+                    pl.semaphore_signal(
+                        ready_sem.at[z], inc=1, device_id=device(level, spot), device_id_type=MESH)
+
+    def send_mate(zz):
         dest = zz * ROW_CHIPS + (col + 1) % ROW_CHIPS
         pltpu.make_async_remote_copy(
             src_ref=send.at[pl.ds(dest * MAXP, MAXP)],
@@ -236,43 +230,123 @@
             recv_sem=recv_sem,
             device_id={"seq": dest},
             device_id_type=MESH).start()
+
+    def forward(away):
+        size, direct = spilled[away], kept_direct(away)
+        rest = MAXP - direct
+        if not size:
+            return
+
+        near = spill_starts(own_first, direct)
+        level = jnp.where(upper == 1, mid - 1 - away, mid + away)
+        source = level * ROW_CHIPS + col
+        whole(landed[away].at[pl.ds(0, size)], spill_sem.at[away]).wait()
+        for j in range(half):
+            for k in range(rest):
+                at = jnp.where(k + direct < near[j][1], near[j][0] + k, size)
+                relay[away, j * rest + k] = landed[away][at]
+        kept = columns(source, direct, rest)
+        for j in range(half):
+            @pl.when(own_first + j != me)
+            def _():
+                pltpu.make_async_remote_copy(
+                    src_ref=relay.at[away, pl.ds(j * rest, rest)],
+                    dst_ref=kept,
+                    send_sem=rsend_sem,
+                    recv_sem=recv_sem,
+                    device_id={"seq": own_first + j},
+                    device_id_type=MESH).start()
+        at_source = pl.ds(pl.multiple_of(source * piece, LANES), piece)
+        for k in range(rest):
+            out[direct + k, :, at_source] = relay[away, (me - own_first) * rest + k]
+
+    def issue(zz, item):
+        if item == SPILL:
+            send_spill(zz, mid - 1 if zz >= mid else mid)
+        elif item == RELAY:
+            for away in range(mid - 1, -1, -1):
+                forward(away)
+        elif item // ROW_CHIPS == zz:
+            send_mate(zz)
+        else:
+            send_piece(zz, item // ROW_CHIPS, item % ROW_CHIPS)
+
+    def issue_early(zz):
+        for s in range(row):
+            @pl.when(jnp.logical_and(z == zz, place_in_row == s))
+            def _():
+                for item in ORDER[zz][s][:EARLY[zz]]:
+                    issue(zz, item)
+
+    def sends_later(zz):
+        for level in range(zz):
+            send_parts(level)
+        if zz == mid:
+            for j in range(1, subs):
+                send_part(zz, col * subs + (sub + j) % subs)
+        else:
+            for j in range(1, row):
+                send_part(zz, (place_in_row + j) % row)
         if zz == mid - 1:
             send_parts(mid)
-        if 0 < zz < mid:
-            send_row(zz, 0)
-        first = mid if zz >= mid else 1
-        for level in range(zz - 1, first - 1, -1):
-            send_row(zz, level)
-        if zz >= mid:
-            for level in range(1, mid):
-                send_row(zz, level)
-        for level in range(zz + 1, line):
-            if (zz, level) != (mid - 1, mid):
-                pl.semaphore_wait(ready_sem.at[level], row)
-                send_parts(level)
-            if level < mid:
-                send_piece(zz, level, 0)
-            elif zz >= mid or level > mid:
-                send_row(zz, level)
-            elif zz != mid - 1:
-                send_spill(zz, mid)
-        for level in range(zz + 1, mid):
-            send_piece(zz, level, 1)
-        if zz < mid - 1:
-            send_row(zz, mid)
-
-    pl.semaphore_wait(barrier, (z + 1) * row - 1 + jnp.where(z == mid - 1, row, 0))
-    for level in range(line - 1):
-        @pl.when(jnp.logical_and(level < z, jnp.logical_not(early(level))))
-        def _():
-            for spot in range(row):
+        for s in range(row):
+            @pl.when(place_in_row == s)
+            def _():
+                known = zz + 1 if zz == mid - 1 else zz
+                for item in ORDER[zz][s][EARLY[zz]:]:
+                    target = zz if item == RELAY else mid if item == SPILL and zz < mid else 0 if item == SPILL else item // ROW_CHIPS
+                    if (zz, target) == (mid, mid) and item != RELAY:
+                        target = mid + 1
+                    while known < target:
+                        known += 1
+                        if (zz, known) != (mid - 1, mid):
+                            pl.semaphore_wait(ready_sem.at[known], row)
+                            send_parts(known)
+                            if (zz, known) == (mid, mid + 1):
+                                for spot in range(subs):
+                                    send_part(zz, (1 - col) * subs + spot)
+                    issue(zz, item)
+
+    for turn in range(2):
+        fill(turn)
+    greeted = z * row + row - 1 + jnp.where(z == mid - 1, subs, 0)
+    pl.semaphore_wait(barrier, jnp.where(z == mid, z * subs + subs - 1, greeted))
+
+    for level in (mid - 1, mid):
+        issue_early(level)
+
+    @pl.when(z == mid - 1)
+    def _():
+        for spot in range(subs):
+            for level, place in ((mid, col), (mid - 1, 1 - col)):
                 pl.semaphore_signal(
-                    ready_sem.at[z], inc=1, device_id=device(level, spot), device_id_type=MESH)
+                    mate_sem, inc=1, device_id=device(level, place * subs + spot),
+                    device_id_type=MESH)
+
+    @pl.when(z != mid)
+    def _():
+        tell_lower()
+
+    for turn in range(2, n):
+        fill(turn)
 
     for level in range(line):
+        size, direct = spilled[away_of(level)], kept_direct(away_of(level))
+        if not size:
+            continue
+
         @pl.when(z == level)
         def _():
-            sends_first(level)
+            far = spill_starts(far_first, direct)
+            for o in range(size):
+                at = direct + o
+                for j in range(1, half):
+                    at = jnp.where(o >= far[j][0], j * MAXP + direct + o - far[j][0], at)
+                spill[o] = send[far_first * MAXP + jnp.minimum(at, half * MAXP - 1)]
+
+    for level in range(line):
+        if level not in (mid - 1, mid):
+            issue_early(level)
 
     lane = lax.broadcasted_iota(jnp.int32, (layers, LANES), 1)
     for dest in range(n):
@@ -287,41 +361,18 @@
         out[k, :, mine] = send[me * MAXP + k]
     parts_in[own_id] = part[me]
 
+    @pl.when(central)
+    def _():
+        pl.semaphore_wait(mate_sem, subs)
+
+    @pl.when(z == mid)
+    def _():
+        tell_lower()
+
     for level in range(line):
         @pl.when(z == level)
         def _():
             sends_later(level)
-
-    for away in range(mid - 1, -1, -1):
-        size, direct = spilled[away], kept_direct(away)
-        rest = MAXP - direct
-        if not size:
-            continue
-
-        @pl.when(relays)
-        def _():
-            near = spill_starts(own_first, direct)
-            level = jnp.where(upper == 1, mid - 1 - away, mid + away)
-            source = level * ROW_CHIPS + col
-            whole(landed[away].at[pl.ds(0, size)], spill_sem.at[away]).wait()
-            for j in range(half):
-                for k in range(rest):
-                    at = jnp.where(k + direct < near[j][1], near[j][0] + k, size)
-                    relay[away, j * rest + k] = landed[away][at]
-            kept = columns(source, direct, rest)
-            for j in range(half):
-                @pl.when(own_first + j != me)
-                def _():
-                    pltpu.make_async_remote_copy(
-                        src_ref=relay.at[away, pl.ds(j * rest, rest)],
-                        dst_ref=kept,
-                        send_sem=rsend_sem,
-                        recv_sem=recv_sem,
-                        device_id={"seq": own_first + j},
-                        device_id_type=MESH).start()
-            at_source = pl.ds(pl.multiple_of(source * piece, LANES), piece)
-            for k in range(rest):
-                out[direct + k, :, at_source] = relay[away, (me - own_first) * rest + k]
 
     others = n * subs - 1
     whole(parts_in.at[pl.ds(0, others)], precv_sem).wait()
@@ -378,6 +429,7 @@
             pltpu.SemaphoreType.DMA,
             pltpu.SemaphoreType.DMA,
             pltpu.SemaphoreType.REGULAR((n // ROW_CHIPS,)),
+            pltpu.SemaphoreType.REGULAR,
             pltpu.SemaphoreType.DMA((4,)),
             pltpu.VMEM(cache_in.shape, cache_in.dtype),
             pltpu.SMEM(page_counts.shape, jnp.int32),
@@ -401,7 +453,7 @@
 
 def shards(cache_in, page_counts, tail_tokens, assignment):
     piece = cache_in.shape[2]
-    whole_tiles = piece % LANES == 0 and piece % LATENT == 0 and lax.axis_size("seq") % (2 * ROW_CHIPS) == 0
+    whole_tiles = piece % LANES == 0 and piece % LATENT == 0 and lax.axis_size("seq") == len(ORDER) * ROW_CHIPS
     return (direct if whole_tiles else general)(cache_in, page_counts, tail_tokens, assignment)
 
 

time: 18.2 us -> 17.4 us (0.956)
  Pallas kernels: 17.4 us -> 16.6 us
    pallas_call x1, Pallas kernels: 16.5 us -> 15.8 us  [direct(): pl.pallas_call(functools.partial(exchange, n, subs), out_shape=(pltpu.VME...]
where the time goes in v3:
time: 17.4 us; the launch traced here: 17.2 us
  Pallas kernels  16.6 us (95%)
  between operations  0.64 us (4%)
    pallas_call x1, Pallas kernels, direct(): pl.pallas_call(functools.partial(exchange, n, subs), out_shape=(pltpu.VME...  15.8 us
    pallas_call x1, Pallas kernels, direct(): pl.pallas_call(place, out_shape=tuple((jax.ShapeDtypeStruct(a.shape, a.dt...  0.84 us

profile of v3, /device:TPU:8, one launch (start us, length us, event | category | flops | bytes accessed | tf_op | source)
XLA Modules:
  0.0 17.2 jit_solution(3809103443605186982)
XLA Ops:
  0.6 15.8 %shard_map.59 = (bf16[8,2,18432]{2,1,0:T(2,128)(2,1)S(1)}, f32[2,8]{1,0:T(2,128)S(1)}) custom-call(s32[8]{0:T(128)} %counts_in.1, s32[8]{0:T(128)} %tails_in.1, s32[8]{0:T(128)} %assign_in.1, bf16[32,2,2304]{2,1,0:T(2,128)(2,1)} %x_in.1), custom_call_target="tpu_custom_call" | custom-call | tf_op jit(solution)/shard_map/pallas_call | solution.py:416
  16.4 0.8 %shard_map.60 = (bf16[8,2,18432]{2,1,0:T(2,128)(2,1)}, f32[2,8]{1,0:T(2,128)}) custom-call(bf16[8,2,18432]{2,1,0:T(2,128)(2,1)S(1)} %get-tuple-element.4.pages_in, f32[2,8]{1,0:T(2,128)S(1)} %get-tuple-element.5.sums_in), custom_call_target="tpu_custom_call" | custom-call | tf_op jit(solution)/shard_map/pallas_call | solution.py:445

commit v4 on v3

--- a/solution.py
+++ b/solution.py
@@ -1,4 +1,5 @@
 import functools
+import math
 
 import jax
 import jax.numpy as jnp
@@ -12,10 +13,14 @@
 MAXP = 8
 LANES = 128
 ROW_CHIPS = 2
-NEAR_DIRECT = 8
-FAR_DIRECT = 4
+DIRECT = 4
 SPILL, RELAY = 8, 9
-ORDER = [[[1, 3, 8, 7, 6, 2, 5, 4], [1, 2, 8, 6, 7, 3, 4, 5], [0, 2, 8, 6, 7, 3, 4, 5], [0, 3, 8, 7, 6, 2, 5, 4]], [[4, 5, 3, 0, 7, 6, 9, 1], [4, 5, 3, 0, 6, 7, 9, 1], [5, 4, 2, 0, 6, 7, 9, 1], [5, 4, 2, 0, 7, 6, 9, 1]], [[0, 1, 3, 2, 7, 6, 5, 9], [0, 1, 3, 2, 6, 7, 5, 9], [1, 0, 2, 3, 6, 7, 4, 9], [1, 0, 2, 3, 7, 6, 4, 9]], [[8, 0, 1, 7, 5, 4, 3, 2], [8, 0, 1, 7, 4, 5, 2, 3], [8, 0, 1, 6, 4, 5, 2, 3], [8, 0, 1, 6, 5, 4, 3, 2]]]
+ORDER = [
+    [[1, 3, 8, 7, 6, 2, 5, 4], [1, 2, 8, 6, 7, 3, 4, 5], [0, 2, 8, 6, 7, 3, 4, 5], [0, 3, 8, 7, 6, 2, 5, 4]],
+    [[4, 5, 3, 0, 7, 6, 9, 1], [4, 5, 3, 0, 6, 7, 9, 1], [5, 4, 2, 0, 6, 7, 9, 1], [5, 4, 2, 0, 7, 6, 9, 1]],
+    [[0, 1, 3, 2, 7, 6, 5, 9], [0, 1, 3, 2, 6, 7, 5, 9], [1, 0, 2, 3, 6, 7, 4, 9], [1, 0, 2, 3, 7, 6, 4, 9]],
+    [[8, 0, 1, 7, 5, 4, 3, 2], [8, 0, 1, 7, 4, 5, 2, 3], [8, 0, 1, 6, 4, 5, 2, 3], [8, 0, 1, 6, 5, 4, 3, 2]],
+]
 EARLY = [0, 1, 1, 3]
 MESH = pl.DeviceIdType.MESH
 
@@ -57,19 +62,18 @@
 
 
 def kept_direct(away):
-    return FAR_DIRECT if away else NEAR_DIRECT
-
-
-def most_spilled(pages, n, direct):
+    return DIRECT if away else MAXP
+
+
+def most_spilled(pages, n):
     half = n // 2
-    room = min(pages - half, half * MAXP)
-    full, rest = room // MAXP, room % MAXP
-    return (MAXP - direct) * full + max(0, rest - direct)
+    full, rest = divmod(min(pages - half, half * MAXP), MAXP)
+    return (MAXP - DIRECT) * full + max(0, rest - DIRECT)
 
 
 def exchange(n, subs, counts_in, tails_in, assign_in, x_in, out, chk, send, tab, part, parts_in,
-             send_sem, recv_sem, psend_sem, precv_sem, ready_sem, mate_sem, in_sem,
-             x, counts, tails, assign, rsend_sem, spill_sem, relay, *spills):
+             send_sem, recv_sem, precv_sem, ready_sem, mate_sem,
+             x, counts, tails, assign, spill_sem, relay, spill, *landed):
     me = lax.axis_index("seq")
     sub = lax.axis_index("sub")
     pages, layers, piece = x.shape
@@ -77,8 +81,8 @@
     line = n // ROW_CHIPS
     mid = line // 2
     half = mid * ROW_CHIPS
-    spilled = [most_spilled(pages, n, kept_direct(away)) for away in range(mid)]
-    spill, landed = spills[0], spills[1:]
+    spilled = spill.shape[0]
+    rest = MAXP - DIRECT
     row = ROW_CHIPS * subs
     z, col = me // ROW_CHIPS, me % ROW_CHIPS
     place_in_row = col * subs + sub
@@ -91,15 +95,26 @@
     def device(level, spot):
         return {"seq": level * ROW_CHIPS + spot // subs, "sub": spot % subs}
 
-    arrivals = [pltpu.make_async_copy(a, b, in_sem.at[k]) for k, (a, b) in enumerate(
-        ((counts_in, counts), (tails_in, tails), (assign_in, assign), (x_in, x)))]
-    for copy in arrivals:
-        copy.start()
     barrier = pltpu.get_barrier_semaphore()
+
     def greet(level, spot):
         pl.semaphore_signal(
             barrier, inc=1, device_id=device(level, spot), device_id_type=MESH)
 
+    @pl.when(z == mid)
+    def _():
+        for spot in range(subs):
+            greet(mid - 1, col * subs + spot)
+
+    arrivals = [pltpu.make_async_copy(a, b, send_sem) for a, b in (
+        (counts_in, counts), (tails_in, tails), (assign_in, assign), (x_in, x))]
+    cuts = math.gcd(pages, 8)
+    cut = pages // cuts
+    for i in range(cuts):
+        part_of = pl.ds(i * cut, cut)
+        pltpu.make_async_copy(x_in.at[part_of], x.at[part_of], send_sem).start()
+    for copy in arrivals[:3]:
+        copy.start()
     for level in range(line):
         @pl.when(z < level)
         def _():
@@ -108,8 +123,6 @@
 
     @pl.when(z == mid)
     def _():
-        for spot in range(subs):
-            greet(mid - 1, col * subs + spot)
         for j in range(1, subs):
             greet(z, col * subs + (sub + j) % subs)
 
@@ -121,8 +134,8 @@
     column = lax.broadcasted_iota(jnp.int32, (layers, piece), 1)
     for f in range(tokens + 1):
         tab[f] = jnp.where(column < f * LATENT, 1.0, 0.0).astype(x.dtype)
-    for away in range(mid):
-        landed[away][spilled[away]] = jnp.zeros((layers, piece), x.dtype)
+    for buffer in landed:
+        buffer[spilled] = jnp.zeros((layers, piece), x.dtype)
 
     for copy in arrivals:
         copy.wait()
@@ -160,12 +173,12 @@
     def away_of(level):
         return level - mid if level >= mid else mid - 1 - level
 
-    def spill_starts(first, direct):
+    def spill_starts(first):
         starts, begin = [], jnp.int32(0)
         for j in range(half):
             count = (request_of(first + j) >> 7) & 15
             starts.append((begin, count))
-            begin = begin + jnp.maximum(count - direct, 0)
+            begin = begin + jnp.maximum(count - DIRECT, 0)
         return starts
 
     def columns(source, first=0, rows=MAXP):
@@ -185,26 +198,21 @@
             device_id={"seq": dest},
             device_id_type=MESH).start()
 
-    def send_row(zz, level):
-        for turn in range(ROW_CHIPS):
-            send_piece(zz, level, (col + 1 + sub + turn) % ROW_CHIPS)
-
-    def send_spill(zz, level):
+    def send_spill(zz):
         away = away_of(zz)
-        if spilled[away]:
-            pltpu.make_async_remote_copy(
-                src_ref=spill.at[pl.ds(0, spilled[away])],
-                dst_ref=landed[away].at[pl.ds(0, spilled[away])],
-                send_sem=send_sem,
-                recv_sem=spill_sem.at[away],
-                device_id={"seq": level * ROW_CHIPS + col},
-                device_id_type=MESH).start()
+        pltpu.make_async_remote_copy(
+            src_ref=spill,
+            dst_ref=landed[away - 1].at[pl.ds(0, spilled)],
+            send_sem=send_sem,
+            recv_sem=spill_sem.at[away - 1],
+            device_id={"seq": (mid - 1 if zz >= mid else mid) * ROW_CHIPS + col},
+            device_id_type=MESH).start()
 
     def send_part(level, spot):
         pltpu.make_async_remote_copy(
             src_ref=part.at[level * ROW_CHIPS + spot // subs],
             dst_ref=parts_in.at[own_id],
-            send_sem=psend_sem,
+            send_sem=send_sem,
             recv_sem=precv_sem,
             device_id=device(level, spot),
             device_id_type=MESH).start()
@@ -215,11 +223,13 @@
 
     def tell_lower():
         for level in range(line - 1):
-            @pl.when(jnp.logical_and(level < z, jnp.logical_not(jnp.logical_and(level == mid - 1, z == mid))))
+            by_entry = jnp.logical_and(level == mid - 1, z == mid)
+
+            @pl.when(jnp.logical_and(level < z, jnp.logical_not(by_entry)))
             def _():
                 for spot in range(row):
                     pl.semaphore_signal(
-                        ready_sem.at[z], inc=1, device_id=device(level, spot), device_id_type=MESH)
+                        ready_sem.at[z - 1], inc=1, device_id=device(level, spot), device_id_type=MESH)
 
     def send_mate(zz):
         dest = zz * ROW_CHIPS + (col + 1) % ROW_CHIPS
@@ -232,39 +242,34 @@
             device_id_type=MESH).start()
 
     def forward(away):
-        size, direct = spilled[away], kept_direct(away)
-        rest = MAXP - direct
-        if not size:
-            return
-
-        near = spill_starts(own_first, direct)
+        near = spill_starts(own_first)
         level = jnp.where(upper == 1, mid - 1 - away, mid + away)
         source = level * ROW_CHIPS + col
-        whole(landed[away].at[pl.ds(0, size)], spill_sem.at[away]).wait()
+        whole(landed[away - 1].at[pl.ds(0, spilled)], spill_sem.at[away - 1]).wait()
         for j in range(half):
             for k in range(rest):
-                at = jnp.where(k + direct < near[j][1], near[j][0] + k, size)
-                relay[away, j * rest + k] = landed[away][at]
-        kept = columns(source, direct, rest)
+                at = jnp.where(k + DIRECT < near[j][1], near[j][0] + k, spilled)
+                relay[away - 1, j * rest + k] = landed[away - 1][at]
+        kept = columns(source, DIRECT, rest)
         for j in range(half):
             @pl.when(own_first + j != me)
             def _():
                 pltpu.make_async_remote_copy(
-                    src_ref=relay.at[away, pl.ds(j * rest, rest)],
+                    src_ref=relay.at[away - 1, pl.ds(j * rest, rest)],
                     dst_ref=kept,
-                    send_sem=rsend_sem,
+                    send_sem=send_sem,
                     recv_sem=recv_sem,
                     device_id={"seq": own_first + j},
                     device_id_type=MESH).start()
         at_source = pl.ds(pl.multiple_of(source * piece, LANES), piece)
         for k in range(rest):
-            out[direct + k, :, at_source] = relay[away, (me - own_first) * rest + k]
+            out[DIRECT + k, :, at_source] = relay[away - 1, (me - own_first) * rest + k]
 
     def issue(zz, item):
         if item == SPILL:
-            send_spill(zz, mid - 1 if zz >= mid else mid)
+            send_spill(zz)
         elif item == RELAY:
-            for away in range(mid - 1, -1, -1):
+            for away in range(mid - 1, 0, -1):
                 forward(away)
         elif item // ROW_CHIPS == zz:
             send_mate(zz)
@@ -294,21 +299,43 @@
             def _():
                 known = zz + 1 if zz == mid - 1 else zz
                 for item in ORDER[zz][s][EARLY[zz]:]:
-                    target = zz if item == RELAY else mid if item == SPILL and zz < mid else 0 if item == SPILL else item // ROW_CHIPS
-                    if (zz, target) == (mid, mid) and item != RELAY:
+                    target = item // ROW_CHIPS
+                    if item == RELAY:
+                        target = zz
+                    elif item == SPILL:
+                        target = mid if zz < mid else 0
+                    elif zz == target == mid:
                         target = mid + 1
                     while known < target:
                         known += 1
                         if (zz, known) != (mid - 1, mid):
-                            pl.semaphore_wait(ready_sem.at[known], row)
+                            pl.semaphore_wait(ready_sem.at[known - 1], row)
                             send_parts(known)
                             if (zz, known) == (mid, mid + 1):
                                 for spot in range(subs):
                                     send_part(zz, (1 - col) * subs + spot)
                     issue(zz, item)
 
+    def pack_rest():
+        for turn in range(2, n):
+            fill(turn)
+
+        @pl.when(jnp.logical_not(central))
+        def _():
+            far = spill_starts(far_first)
+            for o in range(spilled):
+                at = DIRECT + o
+                for j in range(1, half):
+                    at = jnp.where(o >= far[j][0], j * MAXP + DIRECT + o - far[j][0], at)
+                spill[o] = send[far_first * MAXP + jnp.minimum(at, half * MAXP - 1)]
+
     for turn in range(2):
         fill(turn)
+
+    @pl.when(jnp.logical_not(central))
+    def _():
+        pack_rest()
+
     greeted = z * row + row - 1 + jnp.where(z == mid - 1, subs, 0)
     pl.semaphore_wait(barrier, jnp.where(z == mid, z * subs + subs - 1, greeted))
 
@@ -327,23 +354,9 @@
     def _():
         tell_lower()
 
-    for turn in range(2, n):
-        fill(turn)
-
-    for level in range(line):
-        size, direct = spilled[away_of(level)], kept_direct(away_of(level))
-        if not size:
-            continue
-
-        @pl.when(z == level)
-        def _():
-            far = spill_starts(far_first, direct)
-            for o in range(size):
-                at = direct + o
-                for j in range(1, half):
-                    at = jnp.where(o >= far[j][0], j * MAXP + direct + o - far[j][0], at)
-                spill[o] = send[far_first * MAXP + jnp.minimum(at, half * MAXP - 1)]
-
+    @pl.when(central)
+    def _():
+        pack_rest()
     for level in range(line):
         if level not in (mid - 1, mid):
             issue_early(level)
@@ -378,23 +391,20 @@
     whole(parts_in.at[pl.ds(0, others)], precv_sem).wait()
     total = jnp.sum(parts_in[...], axis=0)
     chk[...] = jnp.sqrt(1.0 + total / (PAGE * LATENT))[:, :MAXP]
-    whole(parts_in.at[pl.ds(0, others)], psend_sem).wait()
+    whole(parts_in.at[pl.ds(0, others)], send_sem).wait()
     for level in range(line):
         away = away_of(level)
+        forwards = 0 if away else mid - 1
         sent = (half - 1) * MAXP + half * kept_direct(away)
-        got = (half - 1) * MAXP + half * MAXP
-        if away == 0:
-            got -= sum(MAXP - kept_direct(a) for a in range(mid))
+        got = (n - 1) * MAXP - forwards * rest
 
         @pl.when(z == level)
         def _():
             whole(send.at[pl.ds(0, sent)], send_sem).wait()
-            if spilled[away]:
-                whole(spill.at[pl.ds(0, spilled[away])], send_sem).wait()
-            if away == 0:
-                for a in range(mid):
-                    if spilled[a]:
-                        whole(send.at[pl.ds(0, (half - 1) * (MAXP - kept_direct(a)))], rsend_sem).wait()
+            if away:
+                whole(spill, send_sem).wait()
+            else:
+                whole(send.at[pl.ds(0, forwards * (half - 1) * rest)], send_sem).wait()
             whole(send.at[pl.ds(0, got)], recv_sem).wait()
 
 
@@ -411,7 +421,7 @@
     n, subs = lax.axis_size("seq"), lax.axis_size("sub")
     pages, layers, piece = cache_in.shape
     mid = n // ROW_CHIPS // 2
-    spilled = [most_spilled(pages, n, kept_direct(away)) for away in range(mid)]
+    spilled = most_spilled(pages, n)
     vmem = pl.BlockSpec(memory_space=pltpu.VMEM)
     landed = pl.pallas_call(
         functools.partial(exchange, n, subs),
@@ -427,19 +437,16 @@
             pltpu.SemaphoreType.DMA,
             pltpu.SemaphoreType.DMA,
             pltpu.SemaphoreType.DMA,
-            pltpu.SemaphoreType.DMA,
-            pltpu.SemaphoreType.REGULAR((n // ROW_CHIPS,)),
+            pltpu.SemaphoreType.REGULAR((n // ROW_CHIPS - 1,)),
             pltpu.SemaphoreType.REGULAR,
-            pltpu.SemaphoreType.DMA((4,)),
             pltpu.VMEM(cache_in.shape, cache_in.dtype),
             pltpu.SMEM(page_counts.shape, jnp.int32),
             pltpu.SMEM(page_counts.shape, jnp.int32),
             pltpu.SMEM(page_counts.shape, jnp.int32),
-            pltpu.SemaphoreType.DMA,
-            pltpu.SemaphoreType.DMA((mid,)),
-            pltpu.VMEM((mid, n // 2 * MAXP, layers, piece), cache_in.dtype),
-            pltpu.VMEM((max(spilled) + 1, layers, piece), cache_in.dtype),
-        ] + [pltpu.VMEM((size + 1, layers, piece), cache_in.dtype) for size in spilled],
+            pltpu.SemaphoreType.DMA((mid - 1,)),
+            pltpu.VMEM((mid - 1, n // 2 * (MAXP - DIRECT), layers, piece), cache_in.dtype),
+            pltpu.VMEM((spilled, layers, piece), cache_in.dtype),
+        ] + [pltpu.VMEM((spilled + 1, layers, piece), cache_in.dtype)] * (mid - 1),
         compiler_params=pltpu.CompilerParams(collective_id=0, has_side_effects=True),
     )(page_counts, tail_tokens, assignment, cache_in)
     return pl.pallas_call(
@@ -452,9 +459,12 @@
 
 
 def shards(cache_in, page_counts, tail_tokens, assignment):
-    piece = cache_in.shape[2]
-    whole_tiles = piece % LANES == 0 and piece % LATENT == 0 and lax.axis_size("seq") == len(ORDER) * ROW_CHIPS
-    return (direct if whole_tiles else general)(cache_in, page_counts, tail_tokens, assignment)
+    pages, _, piece = cache_in.shape
+    n, subs = lax.axis_size("seq"), lax.axis_size("sub")
+    whole_tiles = piece % LANES == 0 and piece % LATENT == 0
+    in_order = n == len(ORDER) * ROW_CHIPS and subs * ROW_CHIPS == len(ORDER[0])
+    fits = in_order and page_counts.shape[0] == n
+    return (direct if whole_tiles and fits else general)(cache_in, page_counts, tail_tokens, assignment)
 
 
 def solution(mesh):

time: 17.4 us -> 17.4 us (level)
  no operation moved by 1% of the time
where the time goes in v4:
time: 17.4 us; the launch traced here: 17.1 us
  Pallas kernels  16.5 us (95%)
  between operations  0.64 us (4%)
    pallas_call x1, Pallas kernels, direct(): pl.pallas_call(functools.partial(exchange, n, subs), out_shape=(pltpu.VME...  15.7 us
    pallas_call x1, Pallas kernels, direct(): pl.pallas_call(place, out_shape=tuple((jax.ShapeDtypeStruct(a.shape, a.dt...  0.84 us

profile of v4, /device:TPU:8, one launch (start us, length us, event | category | flops | bytes accessed | tf_op | source)
XLA Modules:
  0.0 17.1 jit_solution(7058925317455201618)
XLA Ops:
  0.6 15.7 %shard_map.59 = (bf16[8,2,18432]{2,1,0:T(2,128)(2,1)S(1)}, f32[2,8]{1,0:T(2,128)S(1)}) custom-call(s32[8]{0:T(128)} %counts_in.1, s32[8]{0:T(128)} %tails_in.1, s32[8]{0:T(128)} %assign_in.1, bf16[32,2,2304]{2,1,0:T(2,128)(2,1)} %x_in.1), custom_call_target="tpu_custom_call" | custom-call | tf_op jit(solution)/shard_map/pallas_call | solution.py:426
  16.3 0.8 %shard_map.60 = (bf16[8,2,18432]{2,1,0:T(2,128)(2,1)}, f32[2,8]{1,0:T(2,128)}) custom-call(bf16[8,2,18432]{2,1,0:T(2,128)(2,1)S(1)} %get-tuple-element.4.pages_in, f32[2,8]{1,0:T(2,128)S(1)} %get-tuple-element.5.sums_in), custom_call_target="tpu_custom_call" | custom-call | tf_op jit(solution)/shard_map/pallas_call | solution.py:452

commit v5 on v4

--- a/solution.py
+++ b/solution.py
@@ -16,8 +16,8 @@
 DIRECT = 4
 SPILL, RELAY = 8, 9
 ORDER = [
-    [[1, 3, 8, 7, 6, 2, 5, 4], [1, 2, 8, 6, 7, 3, 4, 5], [0, 2, 8, 6, 7, 3, 4, 5], [0, 3, 8, 7, 6, 2, 5, 4]],
-    [[4, 5, 3, 0, 7, 6, 9, 1], [4, 5, 3, 0, 6, 7, 9, 1], [5, 4, 2, 0, 6, 7, 9, 1], [5, 4, 2, 0, 7, 6, 9, 1]],
+    [[1, 3, 8, 7, 6, 2, 5, 4], [1, 2, 8, 7, 6, 3, 5, 4], [0, 2, 8, 6, 7, 3, 4, 5], [0, 3, 8, 6, 7, 2, 4, 5]],
+    [[4, 5, 3, 0, 7, 6, 9, 1], [4, 5, 3, 0, 7, 6, 9, 1], [5, 4, 2, 0, 6, 7, 9, 1], [5, 4, 2, 0, 6, 7, 9, 1]],
     [[0, 1, 3, 2, 7, 6, 5, 9], [0, 1, 3, 2, 6, 7, 5, 9], [1, 0, 2, 3, 6, 7, 4, 9], [1, 0, 2, 3, 7, 6, 4, 9]],
     [[8, 0, 1, 7, 5, 4, 3, 2], [8, 0, 1, 7, 4, 5, 2, 3], [8, 0, 1, 6, 4, 5, 2, 3], [8, 0, 1, 6, 5, 4, 3, 2]],
 ]
@@ -72,8 +72,8 @@
 
 
 def exchange(n, subs, counts_in, tails_in, assign_in, x_in, out, chk, send, tab, part, parts_in,
-             send_sem, recv_sem, precv_sem, ready_sem, mate_sem,
-             x, counts, tails, assign, spill_sem, relay, spill, *landed):
+             send_sem, recv_sem, precv_sem, ready_sem, mate_sem, pair_sem,
+             sums, x, counts, tails, assign, spill_sem, relay, spill, *landed):
     me = lax.axis_index("seq")
     sub = lax.axis_index("sub")
     pages, layers, piece = x.shape
@@ -86,7 +86,6 @@
     row = ROW_CHIPS * subs
     z, col = me // ROW_CHIPS, me % ROW_CHIPS
     place_in_row = col * subs + sub
-    own_id = me * subs + sub
     upper = z // mid
     own_first = upper * half
     far_first = half - own_first
@@ -208,18 +207,18 @@
             device_id={"seq": (mid - 1 if zz >= mid else mid) * ROW_CHIPS + col},
             device_id_type=MESH).start()
 
-    def send_part(level, spot):
+    def send_part(level, place):
         pltpu.make_async_remote_copy(
-            src_ref=part.at[level * ROW_CHIPS + spot // subs],
-            dst_ref=parts_in.at[own_id],
+            src_ref=part.at[level * ROW_CHIPS + place],
+            dst_ref=parts_in.at[me],
             send_sem=send_sem,
             recv_sem=precv_sem,
-            device_id=device(level, spot),
+            device_id={"seq": level * ROW_CHIPS + place},
             device_id_type=MESH).start()
 
     def send_parts(level):
-        for spot in range(row):
-            send_part(level, spot)
+        for place in range(ROW_CHIPS):
+            send_part(level, place)
 
     def tell_lower():
         for level in range(line - 1):
@@ -286,12 +285,8 @@
     def sends_later(zz):
         for level in range(zz):
             send_parts(level)
-        if zz == mid:
-            for j in range(1, subs):
-                send_part(zz, col * subs + (sub + j) % subs)
-        else:
-            for j in range(1, row):
-                send_part(zz, (place_in_row + j) % row)
+        if zz != mid:
+            send_part(zz, 1 - col)
         if zz == mid - 1:
             send_parts(mid)
         for s in range(row):
@@ -312,8 +307,7 @@
                             pl.semaphore_wait(ready_sem.at[known - 1], row)
                             send_parts(known)
                             if (zz, known) == (mid, mid + 1):
-                                for spot in range(subs):
-                                    send_part(zz, (1 - col) * subs + spot)
+                                send_part(zz, 1 - col)
                     issue(zz, item)
 
     def pack_rest():
@@ -372,7 +366,7 @@
     mine = pl.ds(pl.multiple_of(me * piece, LANES), piece)
     for k in range(MAXP):
         out[k, :, mine] = send[me * MAXP + k]
-    parts_in[own_id] = part[me]
+    parts_in[me] = part[me]
 
     @pl.when(central)
     def _():
@@ -387,11 +381,20 @@
         def _():
             sends_later(level)
 
-    others = n * subs - 1
-    whole(parts_in.at[pl.ds(0, others)], precv_sem).wait()
-    total = jnp.sum(parts_in[...], axis=0)
+    whole(parts_in.at[pl.ds(0, n - 1)], precv_sem).wait()
+    sums[0] = jnp.sum(parts_in[...], axis=0)
+    pair = pltpu.make_async_remote_copy(
+        src_ref=sums.at[0],
+        dst_ref=sums.at[1],
+        send_sem=send_sem,
+        recv_sem=pair_sem,
+        device_id={"sub": 1 - sub},
+        device_id_type=MESH)
+    pair.start()
+    pair.wait_recv()
+    total = sums[0] + sums[1]
     chk[...] = jnp.sqrt(1.0 + total / (PAGE * LATENT))[:, :MAXP]
-    whole(parts_in.at[pl.ds(0, others)], send_sem).wait()
+    whole(parts_in, send_sem).wait()
     for level in range(line):
         away = away_of(level)
         forwards = 0 if away else mid - 1
@@ -433,12 +436,14 @@
             pltpu.VMEM((n * MAXP, layers, piece), cache_in.dtype),
             pltpu.VMEM((piece // LATENT + 1, layers, piece), cache_in.dtype),
             pltpu.VMEM((n, layers, LANES), jnp.float32),
-            pltpu.VMEM((n * subs, layers, LANES), jnp.float32),
+            pltpu.VMEM((n, layers, LANES), jnp.float32),
             pltpu.SemaphoreType.DMA,
             pltpu.SemaphoreType.DMA,
             pltpu.SemaphoreType.DMA,
             pltpu.SemaphoreType.REGULAR((n // ROW_CHIPS - 1,)),
             pltpu.SemaphoreType.REGULAR,
+            pltpu.SemaphoreType.DMA,
+            pltpu.VMEM((2, layers, LANES), jnp.float32),
             pltpu.VMEM(cache_in.shape, cache_in.dtype),
             pltpu.SMEM(page_counts.shape, jnp.int32),
             pltpu.SMEM(page_counts.shape, jnp.int32),
@@ -462,7 +467,7 @@
     pages, _, piece = cache_in.shape
     n, subs = lax.axis_size("seq"), lax.axis_size("sub")
     whole_tiles = piece % LANES == 0 and piece % LATENT == 0
-    in_order = n == len(ORDER) * ROW_CHIPS and subs * ROW_CHIPS == len(ORDER[0])
+    in_order = n == len(ORDER) * ROW_CHIPS and subs == 2 and subs * ROW_CHIPS == len(ORDER[0])
     fits = in_order and page_counts.shape[0] == n
     return (direct if whole_tiles and fits else general)(cache_in, page_counts, tail_tokens, assignment)
 

time: 17.4 us -> 17.2 us (0.989)
  no operation moved by 1% of the time
where the time goes in v5:
time: 17.2 us; the launch traced here: 17 us
  Pallas kernels  16.4 us (95%)
  between operations  0.64 us (4%)
    pallas_call x1, Pallas kernels, direct(): pl.pallas_call(functools.partial(exchange, n, subs), out_shape=(pltpu.VME...  15.6 us
    pallas_call x1, Pallas kernels, direct(): pl.pallas_call(place, out_shape=tuple((jax.ShapeDtypeStruct(a.shape, a.dt...  0.84 us

profile of v5, /device:TPU:8, one launch (start us, length us, event | category | flops | bytes accessed | tf_op | source)
XLA Modules:
  0.0 17.0 jit_solution(88193847338354777)
XLA Ops:
  0.6 15.6 %shard_map.59 = (bf16[8,2,18432]{2,1,0:T(2,128)(2,1)S(1)}, f32[2,8]{1,0:T(2,128)S(1)}) custom-call(s32[8]{0:T(128)} %counts_in.1, s32[8]{0:T(128)} %tails_in.1, s32[8]{0:T(128)} %assign_in.1, bf16[32,2,2304]{2,1,0:T(2,128)(2,1)} %x_in.1), custom_call_target="tpu_custom_call" | custom-call | tf_op jit(solution)/shard_map/pallas_call | solution.py:429
  16.2 0.8 %shard_map.60 = (bf16[8,2,18432]{2,1,0:T(2,128)(2,1)}, f32[2,8]{1,0:T(2,128)}) custom-call(bf16[8,2,18432]{2,1,0:T(2,128)(2,1)S(1)} %get-tuple-element.4.pages_in, f32[2,8]{1,0:T(2,128)S(1)} %get-tuple-element.5.sums_in), custom_call_target="tpu_custom_call" | custom-call | tf_op jit(solution)/shard_map/pallas_call | solution.py:457

commit v6 on v5

--- a/solution.py
+++ b/solution.py
@@ -21,7 +21,7 @@
     [[0, 1, 3, 2, 7, 6, 5, 9], [0, 1, 3, 2, 6, 7, 5, 9], [1, 0, 2, 3, 6, 7, 4, 9], [1, 0, 2, 3, 7, 6, 4, 9]],
     [[8, 0, 1, 7, 5, 4, 3, 2], [8, 0, 1, 7, 4, 5, 2, 3], [8, 0, 1, 6, 4, 5, 2, 3], [8, 0, 1, 6, 5, 4, 3, 2]],
 ]
-EARLY = [0, 1, 1, 3]
+EARLY = [0, 1, 1, 1]
 MESH = pl.DeviceIdType.MESH
 
 
@@ -72,7 +72,7 @@
 
 
 def exchange(n, subs, counts_in, tails_in, assign_in, x_in, out, chk, send, tab, part, parts_in,
-             send_sem, recv_sem, precv_sem, ready_sem, mate_sem, pair_sem,
+             send_sem, recv_sem, precv_sem, ready_sem, mate_sem, pair_sem, in_sem,
              sums, x, counts, tails, assign, spill_sem, relay, spill, *landed):
     me = lax.axis_index("seq")
     sub = lax.axis_index("sub")
@@ -106,13 +106,14 @@
             greet(mid - 1, col * subs + spot)
 
     arrivals = [pltpu.make_async_copy(a, b, send_sem) for a, b in (
-        (counts_in, counts), (tails_in, tails), (assign_in, assign), (x_in, x))]
+        (counts_in, counts), (tails_in, tails), (assign_in, assign))]
+    pages_here = pltpu.make_async_copy(x_in, x, in_sem)
     cuts = math.gcd(pages, 8)
     cut = pages // cuts
     for i in range(cuts):
         part_of = pl.ds(i * cut, cut)
-        pltpu.make_async_copy(x_in.at[part_of], x.at[part_of], send_sem).start()
-    for copy in arrivals[:3]:
+        pltpu.make_async_copy(x_in.at[part_of], x.at[part_of], in_sem).start()
+    for copy in arrivals:
         copy.start()
     for level in range(line):
         @pl.when(z < level)
@@ -153,9 +154,12 @@
 
     ahead = jnp.where(z == mid - 1, half, 0) + jnp.where(central, col, 0)
 
+    first_two = [request_of((ahead + turn) % n) for turn in range(2)]
+    pages_here.wait()
+
     def fill(turn):
         dest = (ahead + turn) % n
-        info = request_of(dest)
+        info = first_two[turn] if turn < 2 else request_of(dest)
         tail = info & 127
         count = (info >> 7) & 15
         start = info >> 11
@@ -443,6 +447,7 @@
             pltpu.SemaphoreType.REGULAR((n // ROW_CHIPS - 1,)),
             pltpu.SemaphoreType.REGULAR,
             pltpu.SemaphoreType.DMA,
+            pltpu.SemaphoreType.DMA,
             pltpu.VMEM((2, layers, LANES), jnp.float32),
             pltpu.VMEM(cache_in.shape, cache_in.dtype),
             pltpu.SMEM(page_counts.shape, jnp.int32),

time: 17.2 us -> 17.2 us (level)
  no operation moved by 1% of the time
where the time goes in v6:
time: 17.2 us; the launch traced here: 17 us
  Pallas kernels  16.4 us (95%)
  between operations  0.64 us (4%)
    pallas_call x1, Pallas kernels, direct(): pl.pallas_call(functools.partial(exchange, n, subs), out_shape=(pltpu.VME...  15.6 us
    pallas_call x1, Pallas kernels, direct(): pl.pallas_call(place, out_shape=tuple((jax.ShapeDtypeStruct(a.shape, a.dt...  0.84 us

profile of v6, /device:TPU:8, one launch (start us, length us, event | category | flops | bytes accessed | tf_op | source)
XLA Modules:
  0.0 17.0 jit_solution(9991929855329357000)
XLA Ops:
  0.6 15.6 %shard_map.59 = (bf16[8,2,18432]{2,1,0:T(2,128)(2,1)S(1)}, f32[2,8]{1,0:T(2,128)S(1)}) custom-call(s32[8]{0:T(128)} %counts_in.1, s32[8]{0:T(128)} %tails_in.1, s32[8]{0:T(128)} %assign_in.1, bf16[32,2,2304]{2,1,0:T(2,128)(2,1)} %x_in.1), custom_call_target="tpu_custom_call" | custom-call | tf_op jit(solution)/shard_map/pallas_call | solution.py:433
  16.2 0.8 %shard_map.60 = (bf16[8,2,18432]{2,1,0:T(2,128)(2,1)}, f32[2,8]{1,0:T(2,128)}) custom-call(bf16[8,2,18432]{2,1,0:T(2,128)(2,1)S(1)} %get-tuple-element.4.pages_in, f32[2,8]{1,0:T(2,128)S(1)} %get-tuple-element.5.sums_in), custom_call_target="tpu_custom_call" | custom-call | tf_op jit(solution)/shard_map/pallas_call | solution.py:462

commit v7 on v5

--- a/solution.py
+++ b/solution.py
@@ -412,8 +412,8 @@
 
 
 def place(pages_in, sums_in, pages, sums, sem):
-    copies = [pltpu.make_async_copy(a, b, sem.at[k]) for k, (a, b) in enumerate(
-        ((pages_in, pages), (sums_in, sums)))]
+    copies = [pltpu.make_async_copy(a, b, sem) for a, b in (
+        (pages_in, pages), (sums_in, sums))]
     for copy in copies:
         copy.start()
     for copy in copies:
@@ -459,7 +459,7 @@
         out_shape=tuple(jax.ShapeDtypeStruct(a.shape, a.dtype) for a in landed),
         in_specs=[vmem] * 2,
         out_specs=(pl.BlockSpec(memory_space=pltpu.HBM),) * 2,
-        scratch_shapes=[pltpu.SemaphoreType.DMA((2,))],
+        scratch_shapes=[pltpu.SemaphoreType.DMA],
     )(*(pltpu.with_memory_space_constraint(a, pltpu.VMEM) for a in landed))
 
 

time: 17.2 us -> 17.2 us (level)
  no operation moved by 1% of the time
where the time goes in v7:
time: 17.2 us; the launch traced here: 17 us
  Pallas kernels  16.4 us (95%)
  between operations  0.64 us (4%)
    pallas_call x1, Pallas kernels, direct(): pl.pallas_call(functools.partial(exchange, n, subs), out_shape=(pltpu.VME...  15.6 us
    pallas_call x1, Pallas kernels, direct(): pl.pallas_call(place, out_shape=tuple((jax.ShapeDtypeStruct(a.shape, a.dt...  0.83 us

profile of v7, /device:TPU:8, one launch (start us, length us, event | category | flops | bytes accessed | tf_op | source)
XLA Modules:
  0.0 17.0 jit_solution(5249679200881190401)
XLA Ops:
  0.6 15.6 %shard_map.59 = (bf16[8,2,18432]{2,1,0:T(2,128)(2,1)S(1)}, f32[2,8]{1,0:T(2,128)S(1)}) custom-call(s32[8]{0:T(128)} %counts_in.1, s32[8]{0:T(128)} %tails_in.1, s32[8]{0:T(128)} %assign_in.1, bf16[32,2,2304]{2,1,0:T(2,128)(2,1)} %x_in.1), custom_call_target="tpu_custom_call" | custom-call | tf_op jit(solution)/shard_map/pallas_call | solution.py:429
  16.2 0.8 %shard_map.60 = (bf16[8,2,18432]{2,1,0:T(2,128)(2,1)}, f32[2,8]{1,0:T(2,128)}) custom-call(bf16[8,2,18432]{2,1,0:T(2,128)(2,1)S(1)} %get-tuple-element.4.pages_in, f32[2,8]{1,0:T(2,128)S(1)} %get-tuple-element.5.sums_in), custom_call_target="tpu_custom_call" | custom-call | tf_op jit(solution)/shard_map/pallas_call | solution.py:457
